TPU v7x, 512 devices: a whole 4x8x8 slice. The times are simulated.
512 devices in a mesh: frame: 32 (over y_lo, z, core), space: 16 (over x, y_hi).
Axes of the slice: x: 4, y: 8 (y_hi: 4, y_lo: 2; y = y_hi * 2 + y_lo), z: 8, core: 2. Of those that a mesh axis runs over, the one named last changes fastest.
Arguments:
- spatial_query: bfloat16 [32, 1024, 1152], P('frame', 'space'), may hold values from -24 to 24
- spatial_key: bfloat16 [32, 1024, 1152], P('frame', 'space'), may hold values from -24 to 24
- spatial_value: bfloat16 [32, 1024, 1152], P('frame', 'space'), may hold values from -6 to 6
- latents: bfloat16 [32, 1024, 1152], P('frame', 'space'), may hold values from -6 to 6
- proj_weight: bfloat16 [1152, 1152], P('frame'), may hold values from -0.1875 to 0.1875
- proj_bias: float32 [1152], replicated, may hold values from -3 to 3
- residual_gate: float32 [1152], replicated, may hold values from 0.5 to 1.5
- temporal_shift: float32 [1152], replicated, may hold values from -3 to 3
- temporal_scale: float32 [1152], replicated, may hold values from -0.5 to 0.5
- temporal_weight: bfloat16 [1152, 3456], P('frame'), may hold values from -0.75 to 0.75
- clip_lengths: int32 [16], replicated, may hold values from 1 to 4, 32 in all
Outputs:
- hidden: float32 [32, 1024, 1152], P('frame', 'space')
- temporal_out: float32 [32, 1024, 1152], P('frame', 'space')
Inputs may be any that keep to these rules, and one draw needn't show every extreme that they name: `clip_lengths`: 16 clips fill the 32 frames in order; one clip has exactly 4 frames.
All inputs are finite; a program needn't handle non-finite values.
Results may differ from a plain program's by a relative error of at most 0.012.
Values may be sent and summed in bfloat16 or wider, within the bound.
A program may use at most 64 MiB of HBM per device.

v0:
```python
import math

import jax
import jax.numpy as jnp
from jax import lax
from jax.sharding import Mesh
from jax.sharding import PartitionSpec as P

HEADS = 16
FRAME = ("frame_0", "frame_1", "frame_2")


neg_fill = -1e30


def in_blocks(shard, dim, devices):
    before, after = (shard.shape[:dim], shard.shape[dim + 1 :])
    return jnp.moveaxis(shard.reshape(*before, devices, -1, *after), dim, 0)


def in_order(blocks, dim):
    shape = list(blocks.shape[1:])
    shape[dim] *= blocks.shape[0]
    return jnp.moveaxis(blocks, 0, dim).reshape(shape)


def exchange_in_order(blocks, axes, sequence):
    shape = [lax.axis_size(a) for a in axes]
    blocks = blocks.reshape(*shape, *blocks.shape[1:])
    for k in sequence:
        blocks = lax.all_to_all(blocks, axes[k], split_axis=k, concat_axis=k, tiled=True)
    return blocks.reshape(-1, *blocks.shape[len(axes) :])


def exchange_by_chip(shard, groups, sequence, split_dim, concat_dim):
    devices = lax.axis_size(groups[0]) * lax.axis_size(groups[1])
    blocks = in_blocks(shard, split_dim, devices)
    return in_order(exchange_in_order(blocks, groups, sequence), concat_dim)


def head_scores(query, keys):
    factor = 1.0 / math.sqrt(query.shape[-1])
    return jnp.einsum("fahd,fbhd->fhab", query, keys, preferred_element_type=jnp.float32) * factor


def frame_attention(parts):
    query, keys, values = parts
    frames, count, heads, head_dim = query.shape
    block = math.gcd(count, 512)
    blocks = jnp.moveaxis(query.reshape(frames, count // block, block, heads, head_dim), 1, 0)

    def one_block(rows):
        scores = head_scores(rows, keys)
        top = jnp.max(scores, axis=-1, keepdims=True)
        probs = jnp.exp(scores - top)
        total = jnp.sum(probs, axis=-1)
        mixed = jnp.einsum(
            "fhab,fbhd->fahd",
            probs.astype(jnp.bfloat16),
            values,
            preferred_element_type=jnp.float32,
        )
        return (mixed / jnp.transpose(total, (0, 2, 1))[..., None]).astype(jnp.bfloat16)

    result = lax.map(one_block, blocks)
    return jnp.moveaxis(result, 0, 1).reshape(frames, count, heads, head_dim)


def temporal_mix(packed, allowed):
    frames, count = (packed.shape[0], packed.shape[1])
    width = packed.shape[2] // 3
    head_dim = width // HEADS
    split = (frames, count, HEADS, head_dim)
    query = packed[:, :, :width].reshape(split)
    keys = packed[:, :, width : 2 * width].reshape(split)
    values = packed[:, :, 2 * width :].reshape(split)
    scores = jnp.einsum("anhd,bnhd->nhab", query, keys, preferred_element_type=jnp.float32) * (
        1.0 / math.sqrt(head_dim)
    )
    scores = jnp.where(allowed, scores, neg_fill)
    top = jnp.max(scores, axis=-1, keepdims=True)
    probs = jnp.exp(scores - top)
    total = jnp.sum(probs, axis=-1)
    mixed = jnp.einsum(
        "nhab,bnhd->anhd", probs.astype(jnp.bfloat16), values, preferred_element_type=jnp.float32
    )
    mixed = mixed / jnp.transpose(total, (2, 0, 1))[..., None]
    return mixed.reshape(frames, count, width)


def shards(
    spatial_query,
    spatial_key,
    spatial_value,
    latents,
    proj_weight,
    proj_bias,
    residual_gate,
    temporal_shift,
    temporal_scale,
    temporal_weight,
    clip_lengths,
):
    frames_dev, patches_dev, width = latents.shape
    head_dim = width // HEADS
    split = (frames_dev, patches_dev, HEADS, head_dim)
    query = spatial_query.reshape(split)
    mixed_heads = frame_attention(
        (
            lax.all_to_all(query, "space", split_axis=2, concat_axis=1, tiled=True),
            lax.all_to_all(
                spatial_key.reshape(split), "space", split_axis=2, concat_axis=1, tiled=True
            ),
            lax.all_to_all(
                spatial_value.reshape(split), "space", split_axis=2, concat_axis=1, tiled=True
            ),
        )
    )
    attended = lax.all_to_all(mixed_heads, "space", split_axis=1, concat_axis=2, tiled=True)
    rows = frames_dev * patches_dev
    flat = attended.reshape(rows, width)
    projected = jnp.dot(
        flat,
        lax.all_gather(proj_weight, FRAME, axis=0, tiled=True),
        preferred_element_type=jnp.float32,
    )
    hidden = latents.reshape(rows, width).astype(jnp.float32) + residual_gate * (
        projected + proj_bias
    )
    mean = jnp.mean(hidden, axis=-1, keepdims=True)
    centred = hidden - mean
    variance = jnp.mean(centred * centred, axis=-1, keepdims=True)
    normed = (
        centred * lax.rsqrt(variance + 1e-06) * (1.0 + temporal_scale) + temporal_shift
    ).astype(jnp.bfloat16)
    groups = lax.axis_size(FRAME)
    frames_all = frames_dev * groups
    per_group = patches_dev // groups
    ends = jnp.cumsum(clip_lengths)
    clip_of = jnp.sum(
        (jnp.arange(frames_all, dtype=jnp.int32)[:, None] >= ends[None, :]).astype(jnp.int32),
        axis=1,
    )
    allowed = clip_of[:, None] == clip_of[None, :]
    whole_weight = lax.all_gather(temporal_weight, FRAME, axis=0, tiled=True)
    local = jnp.einsum(
        "fnc,ce->fne",
        exchange_by_chip(
            normed.reshape(frames_dev, groups, per_group, width),
            (("frame_0", "frame_1"), "frame_2"),
            (1, 0),
            1,
            0,
        )[:, 0],
        whole_weight,
        preferred_element_type=jnp.float32,
    ).astype(jnp.bfloat16)
    temporal = temporal_mix(local, allowed)[:, None]
    temporal = temporal.reshape(frames_all, per_group, width)
    temporal_out = lax.all_to_all(
        temporal.astype(jnp.bfloat16), FRAME, split_axis=0, concat_axis=1, tiled=True
    ).astype(temporal.dtype)
    return (hidden.reshape(frames_dev, patches_dev, width), temporal_out)


def solution(mesh):
    split = Mesh(
        mesh.devices.reshape(2, 8, 2, mesh.shape["space"]),
        ("frame_0", "frame_1", "frame_2", "space"),
    )
    return jax.shard_map(
        shards,
        mesh=split,
        in_specs=(
            P(FRAME, "space", None),
            P(FRAME, "space", None),
            P(FRAME, "space", None),
            P(FRAME, "space", None),
            P(FRAME, None),
            P(),
            P(),
            P(),
            P(),
            P(FRAME, None),
            P(),
        ),
        out_specs=(P(FRAME, "space", None), P(FRAME, "space", None)),
        check_vma=False,
    )
```

profile of v0, /device:TPU:1, one launch (start us, length us, event | category | flops | bytes accessed | tf_op | source)
XLA Modules:
  0.0 205.7 jit_solution(14141695110795643575)
XLA Ops:
  7.2 0.7 all-gather.5.cloned.1.call-update
  8.0 0.7 all-gather.7.cloned.1.call-update
  8.7 1.4 reshape.123
  10.0 0.8 copy.88
  10.8 10.2 %all-to-all-start = ((bf16[1,64,16,72]{3,1,0,2:T(8,128)(2,1)}), bf16[1,64,16,72]{3,1,0,2:T(8,128)(2,1)S(1)}, u32[]{:S(2)}, u32[]{:S(2)}) async-start(bf16[1,64,16,72]{3,1,0,2:T(8,128)(2,1)} %copy.88), calls=%async_computation | async-start | bytes 524288 | tf_op jit(solution)/shard_map/all_to_all | solution.py:110
  21.0 1.4 reshape.124
  22.4 0.8 copy.90
  23.2 10.2 %all-to-all-done = bf16[1,64,16,72]{3,1,0,2:T(8,128)(2,1)S(1)} async-done(((bf16[1,64,16,72]{3,1,0,2:T(8,128)(2,1)}), bf16[1,64,16,72]{3,1,0,2:T(8,128)(2,1)S(1)}, u32[]{:S(2)}, u32[]{:S(2)}) %all-to-all-start) | async-done | bytes 147488 | tf_op jit(solution)/shard_map/all_to_all | solution.py:110
  33.4 3.9 %all-to-all-start.1 = ((bf16[1,64,16,72]{3,1,0,2:T(8,128)(2,1)}), bf16[1,64,16,72]{3,1,0,2:T(8,128)(2,1)S(1)}, u32[]{:S(2)}, u32[]{:S(2)}) async-start(bf16[1,64,16,72]{3,1,0,2:T(8,128)(2,1)} %copy.90), calls=%async_computation.1 | async-start | bytes 524288 | tf_op jit(solution)/shard_map/all_to_all | solution.py:111
  37.3 0.5 reshape.125
  37.7 0.8 copy.92
  38.5 13.1 %all-to-all-done.1 = bf16[1,64,16,72]{3,1,0,2:T(8,128)(2,1)S(1)} async-done(((bf16[1,64,16,72]{3,1,0,2:T(8,128)(2,1)}), bf16[1,64,16,72]{3,1,0,2:T(8,128)(2,1)S(1)}, u32[]{:S(2)}, u32[]{:S(2)}) %all-to-all-start.1) | async-done | bytes 147488 | tf_op jit(solution)/shard_map/all_to_all | solution.py:111
  51.6 3.5 %all-to-all-start.2 = ((bf16[1,64,16,72]{3,1,0,2:T(8,128)(2,1)}), bf16[1,64,16,72]{3,1,0,2:T(8,128)(2,1)S(1)}, u32[]{:S(2)}, u32[]{:S(2)}) async-start(bf16[1,64,16,72]{3,1,0,2:T(8,128)(2,1)} %copy.92), calls=%async_computation.2 | async-start | bytes 524288 | tf_op jit(solution)/shard_map/all_to_all | solution.py:114
  55.4 14.1 %all-to-all-done.2 = bf16[1,64,16,72]{3,1,0,2:T(8,128)(2,1)S(1)} async-done(((bf16[1,64,16,72]{3,1,0,2:T(8,128)(2,1)}), bf16[1,64,16,72]{3,1,0,2:T(8,128)(2,1)S(1)}, u32[]{:S(2)}, u32[]{:S(2)}) %all-to-all-start.2) | async-done | bytes 147488 | tf_op jit(solution)/shard_map/all_to_all | solution.py:114
  69.7 3.4 %while.10 = (s32[]{:T(128)}, bf16[2,1,512,1,72]{2,4,3,1,0:T(8,128)(2,1)S(1)}, bf16[2,1,512,1,72]{2,4,3,1,0:T(8,128)(2,1)S(1)}, bf16[1,1024,1,72]{1,3,2,0:T(8,128...) while((s32[]{:T(128)}, bf16[2,1,512,1,72]{2,4,3,1,0:T(8,128)(2,1)S(1)}, ...), condition=%wide.region_3.4_spmd, body=%wide.region_0.3_spmd.sunk | while | flops 155261952 | bytes 6744149 | solution.py:65
  69.7 0.6 multiply_reduce_fusion.3
  70.3 0.5 fusion.39
  70.8 0.6 fusion.40
  71.4 0.5 multiply_reduce_fusion.3
  71.9 0.5 fusion.39
  72.5 0.6 fusion.40
  73.4 0.5 broadcast.46
  73.9 2.3 %reduce.5 = bf16[1024,72]{1,0:T(8,128)(2,1)S(1)} reduce(bf16[1024,1,1,72]{3,2,1,0:T(2,128)(2,1)S(1)} %bitcast.98, bf16[]{:T(256)} %broadcast.46), dimensions={1,2}, to_apply=%bitcast.78.reduce_sub_computation | reduce | bytes 294914
  76.2 1.2 reshape.144
  77.4 3.5 %all-to-all-start.3 = ((bf16[16,2,2304]{2,1,0:T(2,128)(2,1)}), bf16[16,2,2304]{2,1,0:T(2,128)(2,1)S(1)}, u32[]{:S(2)}, u32[]{:S(2)}) async-start(bf16[16,2,2304]{2,1,0:T(2,128)(2,1)} %reshape.144), calls=%async_computation.3 | async-start | bytes 294912 | tf_op jit(solution)/shard_map/all_to_all | solution.py:119
  81.2 9.5 %all-to-all-done.3 = bf16[16,2,2304]{2,1,0:T(2,128)(2,1)S(1)} async-done(((bf16[16,2,2304]{2,1,0:T(2,128)(2,1)}), bf16[16,2,2304]{2,1,0:T(2,128)(2,1)S(1)}, u32[]{:S(2)}, u32[]{:S(2)}) %all-to-all-start.3) | async-done | bytes 147488 | tf_op jit(solution)/shard_map/all_to_all | solution.py:119
  90.7 0.9 reshape.145
  91.6 0.3 copy.97
  92.0 0.2 all_to_all.73
  92.2 0.4 copy.98
  92.6 0.3 reshape.126
  92.9 3.6 %reshape.136 = bf16[1152,1152]{1,0:T(8,128)(2,1)S(1)} reshape(bf16[32,36,1152]{2,1,0:T(8,128)(2,1)} %all-gather.5.cloned.1.call-done) | data formatting | bytes 5308416
  96.6 0.7 fusion.28
  97.3 0.2 multiply_reduce_fusion.1
  97.8 6.7 %all_to_all.85 = bf16[16,2,1,1,2,1152]{5,4,0,3,2,1:T(2,128)(2,1)S(1)} all-to-all(bf16[16,2,1,1,2,1152]{5,4,0,3,2,1:T(2,128)(2,1)S(1)} %copy.99), channel_id=1, replica_groups=mesh['frame_0'=2,'frame_1'=8,'frame_2'=2,'space'=16] {'frame_2'}, dimensions={1} | all-to-all | bytes 294912 | tf_op jit(solution)/shard_map/all_to_all | solution.py:31
  104.5 0.8 copy.100
  105.3 9.1 %all-to-all-start.5 = ((bf16[16,2,1,1,2,1152]{5,4,1,3,2,0:T(2,128)(2,1)}), bf16[16,2,1,1,2,1152]{5,4,1,3,2,0:T(2,128)(2,1)S(1)}, u32[]{:S(2)}, u32[]{:S(2)}) async-start(bf16[16,2,1,1,2,1152]{5,4,1,3,2,0:T(2,128)(2,1)} %copy.100), calls=%async_computation.5 | async-start | bytes 294912 | tf_op jit(solution)/shard_map/all_to_all | solution.py:31
  114.6 49.2 %all-gather.7.cloned.1.call-done = bf16[32,36,3456]{2,1,0:T(8,128)(2,1)} async-done(((bf16[1,36,3456]{2,1,0:T(8,128)(2,1)}), bf16[32,36,3456]{2,1,0:T(8,128)(2,1)}) %all-gather.7.cloned.1.call-update) | async-done | bytes 7962640 | tf_op jit(solution)/shard_map/all_gather | solution.py:145
  163.8 12.4 %reshape.139 = bf16[1152,3456,1]{1,0,2:T(8,128)(2,1)} reshape(bf16[32,36,3456]{2,1,0:T(8,128)(2,1)} %all-gather.7.cloned.1.call-done) | data formatting | bytes 15925248
  176.2 4.6 %convolution_convert_fusion = bf16[32,2,3456]{2,0,1:T(8,128)(2,1)S(1)} fusion(bf16[1152,3456,1]{1,0,2:T(8,128)(2,1)} %reshape.139, bf16[32,2,1152]{2,1,0:T(2,128)(2,1)S(1)} %bitcast.104), kind=kOutput, calls=%fused_computation.16 | convolution fusion | flops 509829120 | bytes 8552448 | tf_op jit(solution)/shard_map/fnc,ce->fne/dot_general | solution.py:146
  180.8 0.5 reshape.132
  181.3 0.5 reshape.131
  181.7 0.5 reshape.128
  182.2 0.3 fusion.29
  182.6 0.3 fusion.18
  183.1 0.4 reshape.142
  183.5 14.6 %all_to_all.86 = bf16[32,2,1152]{2,1,0:T(2,128)(2,1)S(1)} all-to-all(bf16[32,2,1152]{2,1,0:T(2,128)(2,1)S(1)} %reshape.142), channel_id=1, replica_groups=mesh['frame_0'=2,'frame_1'=8,'frame_2'=2,'space'=16] {'frame_0','frame_1..., dimensions={0} | all-to-all | bytes 294912 | tf_op jit(solution)/shard_map/all_to_all | solution.py:160
  198.1 0.8 reshape.134
  (40 shorter events, 1.8 us)
Async XLA Ops:
  7.2 30.1 %copy-start.1 = (bf16[1,64,1152]{2,1,0:T(8,128)(2,1)S(1)}, bf16[1,64,1152]{2,1,0:T(8,128)(2,1)}, u32[]{:S(2)}) copy-start(bf16[1,64,1152]{2,1,0:T(8,128)(2,1)} %param.15) | copy-start | bytes 442372
  7.2 85.7 %all-gather.5.cloned.1.call-start = ((), (), s32[]{:S(2)}) async-start(), calls=%async_computation.7 | async-start | bytes 3041280 | tf_op jit(solution)/shard_map/all_gather | solution.py:124
  7.9 155.8 %all-gather.7.cloned.1.call-start = ((), (), s32[]{:S(2)}) async-start(), calls=%async_computation.8 | async-start | bytes 9123840 | tf_op jit(solution)/shard_map/all_gather | solution.py:145
  10.8 22.6 %all-to-all-start = ((bf16[1,64,16,72]{3,1,0,2:T(8,128)(2,1)}), bf16[1,64,16,72]{3,1,0,2:T(8,128)(2,1)S(1)}, u32[]{:S(2)}, u32[]{:S(2)}) async-start(bf16[1,64,16,72]{3,1,0,2:T(8,128)(2,1)} %copy.88), calls=%async_computation | async-start | bytes 524288 | tf_op jit(solution)/shard_map/all_to_all | solution.py:110
  33.4 18.2 %all-to-all-start.1 = ((bf16[1,64,16,72]{3,1,0,2:T(8,128)(2,1)}), bf16[1,64,16,72]{3,1,0,2:T(8,128)(2,1)S(1)}, u32[]{:S(2)}, u32[]{:S(2)}) async-start(bf16[1,64,16,72]{3,1,0,2:T(8,128)(2,1)} %copy.90), calls=%async_computation.1 | async-start | bytes 524288 | tf_op jit(solution)/shard_map/all_to_all | solution.py:111
  51.6 18.0 %all-to-all-start.2 = ((bf16[1,64,16,72]{3,1,0,2:T(8,128)(2,1)}), bf16[1,64,16,72]{3,1,0,2:T(8,128)(2,1)S(1)}, u32[]{:S(2)}, u32[]{:S(2)}) async-start(bf16[1,64,16,72]{3,1,0,2:T(8,128)(2,1)} %copy.92), calls=%async_computation.2 | async-start | bytes 524288 | tf_op jit(solution)/shard_map/all_to_all | solution.py:114
  73.1 7.8 %copy-start.7 = (s32[16]{0:T(128)S(1)}, s32[16]{0:T(128)}, u32[]{:S(2)}) copy-start(s32[16]{0:T(128)} %param.23) | copy-start | bytes 196
  73.1 8.1 %copy-start.6 = (f32[1152]{0:T(1024)S(1)}, f32[1152]{0:T(1024)}, u32[]{:S(2)}) copy-start(f32[1152]{0:T(1024)} %param.21) | copy-start | bytes 13828
  77.4 13.3 %all-to-all-start.3 = ((bf16[16,2,2304]{2,1,0:T(2,128)(2,1)}), bf16[16,2,2304]{2,1,0:T(2,128)(2,1)S(1)}, u32[]{:S(2)}, u32[]{:S(2)}) async-start(bf16[16,2,2304]{2,1,0:T(2,128)(2,1)} %reshape.144), calls=%async_computation.3 | async-start | bytes 294912 | tf_op jit(solution)/shard_map/all_to_all | solution.py:119
  92.8 3.7 %copy-start.2 = (bf16[1,64,1152]{2,1,0:T(8,128)(2,1)S(1)}, bf16[1,64,1152]{2,1,0:T(8,128)(2,1)}, u32[]{:S(2)}) copy-start(bf16[1,64,1152]{2,1,0:T(8,128)(2,1)} %param.16) | copy-start | bytes 442372
  92.9 3.7 %copy-start.3 = (f32[1152]{0:T(1024)S(1)}, f32[1152]{0:T(1024)}, u32[]{:S(2)}) copy-start(f32[1152]{0:T(1024)} %param.18) | copy-start | bytes 13828
  92.9 3.7 %copy-start.4 = (f32[1152]{0:T(1024)S(1)}, f32[1152]{0:T(1024)}, u32[]{:S(2)}) copy-start(f32[1152]{0:T(1024)} %param.19) | copy-start | bytes 13828
  96.6 0.9 copy-start.5
  97.3 78.9 %copy-start = (f32[64,1152]{1,0:T(8,128)}, f32[64,1152]{1,0:T(8,128)S(1)}, u32[]{:S(2)}) copy-start(f32[64,1152]{1,0:T(8,128)S(1)} %get-tuple-element.71) | copy-start | bytes 884740
  105.3 70.9 %all-to-all-start.5 = ((bf16[16,2,1,1,2,1152]{5,4,1,3,2,0:T(2,128)(2,1)}), bf16[16,2,1,1,2,1152]{5,4,1,3,2,0:T(2,128)(2,1)S(1)}, u32[]{:S(2)}, u32[]{:S(2)}) async-start(bf16[16,2,1,1,2,1152]{5,4,1,3,2,0:T(2,128)(2,1)} %copy.100), calls=%async_computation.5 | async-start | bytes 294912 | tf_op jit(solution)/shard_map/all_to_all | solution.py:31
Sparse Core Ops, SparseCore 0:
  10.1 74.3 all-gather.4
  86.6 77.0 all-gather.6
where the time goes:
time: 207 us; the launch traced here: 206 us
  waiting for transfers between devices  97.6 us (47%)
  starting transfers between devices  30.3 us (15%)
  local copies, waits for them, and re-layouts  29.8 us (14%)
  blocking collectives  21.3 us (10%)
  between operations  14.4 us (7%)
  matrix products  8.13 us (4%)
  other arithmetic  4.11 us (2%)
    all_gather x1, waiting for transfers between devices, shards(): whole_weight = lax.all_gather(temporal_weight, FRAME, axis=0, tiled=True)  49.2 us
    unnamed x21, local copies, waits for them, and re-layouts  18.7 us
    all_to_all x1, blocking collectives, shards(): lax.all_to_all(temporal.astype(jnp.bfloat16), FRAME, split_axis=0, concat...  14.6 us
    all_to_all x1, waiting for transfers between devices, shards(): lax.all_to_all(spatial_value.reshape(split), 'space', split_axis=2, conca...  14.1 us
    all_to_all x1, waiting for transfers between devices, shards(): lax.all_to_all(spatial_key.reshape(split), 'space', split_axis=2, concat_...  13.1 us
    all_to_all x1, starting transfers between devices, shards(): lax.all_to_all(query, 'space', split_axis=2, concat_axis=1, tiled=True)  10.2 us
    all_to_all x1, waiting for transfers between devices, shards(): lax.all_to_all(query, 'space', split_axis=2, concat_axis=1, tiled=True)  10.2 us
    all_to_all x1, waiting for transfers between devices, shards(): lax.all_to_all(mixed_heads, 'space', split_axis=1, concat_axis=2, tiled=T...  9.53 us
  transfers between devices with their start and end apart: 7, of which 5 were waited for; matrix products, arithmetic and copies ran while one was open for 16% of the time, Pallas kernels for 0%

commit v1 on v0

v1 whole, which is shorter than its diff:
```python
import math

import jax
import jax.numpy as jnp
from jax import lax
from jax.experimental import pallas as pl
from jax.experimental.pallas import tpu as pltpu
from jax.sharding import PartitionSpec as P

MESH = pl.DeviceIdType.MESH
BF = jnp.bfloat16
F32 = jnp.float32

HEADS = 16
HD = 72
D = HEADS * HD
NS = 16
NF = 32
ROWS = 64
NZ = 8
SHARD = 36
QUAD = 4 * SHARD
HALF = D // 2
WT = 3 * HALF
GROUP = 4
TOK = NF * GROUP
NEG = -1e30
LOG2E = 1.4426950408889634

ORDER = tuple((j % 2) * 8 + j // 2 for j in range(HEADS))


def remote(src, dst, send, recv, f, s):
    return pltpu.make_async_remote_copy(
        src_ref=src, dst_ref=dst, send_sem=send, recv_sem=recv, device_id=(f, s), device_id_type=MESH
    )


def kernel(
    clip_ref, q_ref, k_ref, v_ref, lat_ref, wp_ref, wt_ref, bias_ref, gate_ref, shift_ref, scale_ref,
    hidden_ref, out_ref,
    pack, got, att, attgot, wpq, wtq, wp, wt, toks, tokgot, rets, retgot, flat, mask_ref,
    qkv_s, qkv_r, att_s, att_r, tok_s, tok_r, ret_s, ret_r,
    pre_s, pre_r, ring_s, ring_r, die_s, die_r,
):
    f = lax.axis_index("frame")
    s = lax.axis_index("space")
    row = f // 16
    z = (f // 2) % NZ
    c = f % 2
    group = f % 16
    yhi = s % 4
    step = 1 - 2 * c
    fz = row * 16 + ((z + step + NZ) % NZ) * 2 + c
    sib = row * 16 + z * 2 + (1 - c)
    other = (1 - row) * 16 + z * 2 + c
    sb = (s - yhi) + (yhi + 2 * row - 1 + 4) % 4
    me_q = row * 2 + c
    other_q = (1 - row) * 2 + c

    barrier = pltpu.get_barrier_semaphore()

    def hail_space(i, _):
        pl.semaphore_signal(barrier, inc=1, device_id=(f, (s + i) % NS), device_id_type=MESH)
        return 0

    def hail_frame(i, _):
        pl.semaphore_signal(barrier, inc=1, device_id=((f + i) % NF, s), device_id_type=MESH)
        return 0

    lax.fori_loop(1, NS, hail_space, 0)
    lax.fori_loop(1, NF, hail_frame, 0)
    pl.semaphore_signal(barrier, inc=1, device_id=(other, sb), device_id_type=MESH)

    for h in range(HEADS):
        cut = pl.ds(h * HD, HD)
        kk, qq, vv = k_ref[:, cut], q_ref[:, cut], v_ref[:, cut]
        pack[h, :, 0:128] = jnp.concatenate([kk, qq[:, :56]], axis=1)
        pack[h, :, 128:256] = jnp.concatenate([vv, qq[:, 56:], jnp.zeros((ROWS, 40), BF)], axis=1)
    wpq[me_q] = wp_ref[...]
    wtq[me_q] = wt_ref[row]

    pl.semaphore_wait(barrier, NS - 1 + NF - 1 + 1)

    wp_y = remote(wp_ref, wpq.at[me_q], pre_s.at[0], pre_r.at[0], other, sb)
    wp_c = remote(wp_ref, wpq.at[me_q], pre_s.at[1], pre_r.at[1], sib, s)
    wp_y.start()
    wp_c.start()

    def send_qkv(i, _):
        to = (s + i) % NS
        remote(pack.at[to], got.at[s], qkv_s, qkv_r, f, to).start()
        return 0

    lax.fori_loop(1, NS, send_qkv, 0)
    wt_y = remote(wt_ref.at[1 - row], wtq.at[me_q], pre_s.at[2], pre_r.at[2], other, s)
    wt_c = remote(wt_ref.at[row], wtq.at[me_q], pre_s.at[3], pre_r.at[3], sib, s)
    wt_y.start()
    wt_c.start()
    got[s] = pack[s]

    def ring(m, buf, k):
        block = (z - step * k + 2 * NZ) % NZ
        src = buf.at[block] if k < 3 else buf.at[block, pl.ds(pl.multiple_of(c * 64, 16), 80)]
        return remote(src, src, ring_s.at[m * 4 + k], ring_r.at[m * 4 + k], fz, s)

    def ring_arrived(m, buf, k):
        block = (z - step * (k + 1) + 2 * NZ) % NZ
        dst = buf.at[block] if k < 3 else buf.at[block, pl.ds(pl.multiple_of(c * 64, 16), 80)]
        return remote(dst, dst, ring_s.at[m * 4 + k], ring_r.at[m * 4 + k], fz, s)

    def die(m, buf, k):
        block = (z - step * (k + 1) + 2 * NZ) % NZ
        src = buf.at[block] if k < 3 else buf.at[block, pl.ds(pl.multiple_of(c * 80, 16), 64)]
        return remote(src, src, die_s.at[m * 4 + k], die_r.at[m * 4 + k], sib, s)

    def die_arrived(m, buf, k):
        block = (z + step * (k + 1) + 2 * NZ) % NZ
        dst = buf.at[block] if k < 3 else buf.at[block, pl.ds(pl.multiple_of((1 - c) * 80, 16), 64)]
        return remote(dst, dst, die_s.at[m * 4 + k], die_r.at[m * 4 + k], sib, s)

    def relay(m, buf, k):
        ring_arrived(m, buf, k).wait_recv()
        if k < 3:
            ring(m, buf, k + 1).start()
        die(m, buf, k).start()

    def begin(m, quads, buf, over_y, over_c):
        over_y.wait_recv()
        more = remote(quads.at[other_q], quads.at[other_q], pre_s.at[4 + m], pre_r.at[4 + m], sib, s)
        more.start()
        over_c.wait_recv()
        more.wait_recv()
        buf[z] = jnp.concatenate([quads[i].astype(F32) for i in range(4)], axis=0).astype(BF)
        ring(m, buf, 0).start()
        return more

    wp_more = begin(0, wpq, wp, wp_y, wp_c)

    ri = lax.broadcasted_iota(jnp.int32, (TOK, TOK), 0)
    ci = lax.broadcasted_iota(jnp.int32, (TOK, TOK), 1)
    clip_r = jnp.zeros((TOK, TOK), jnp.int32)
    clip_c = jnp.zeros((TOK, TOK), jnp.int32)
    end = jnp.int32(0)
    for i in range(clip_ref.shape[0]):
        end = end + clip_ref[i]
        clip_r = clip_r + jnp.where(ri >= GROUP * end, 1, 0)
        clip_c = clip_c + jnp.where(ci >= GROUP * end, 1, 0)
    same = (clip_r == clip_c) & ((ri % GROUP) == (ci % GROUP))
    mask_ref[...] = jnp.where(same, 1.0, 0.0)

    relay(0, wp, 0)

    def total(buf, n, recv):
        return remote(buf.at[pl.ds(0, n)], buf.at[pl.ds(0, n)], recv, recv, f, s)

    total(got, NS - 1, qkv_r).wait_recv()

    lane = lax.broadcasted_iota(jnp.int32, (NS * ROWS, 128), 1)
    left = got[:, :, 0:128].reshape(NS * ROWS, 128)
    right = got[:, :, 128:256].reshape(NS * ROWS, 128)
    values = jnp.where(lane < HD, right.astype(F32), jnp.where(lane == HD, 1.0, 0.0)).astype(BF)
    qblock = 256
    factor = LOG2E / math.sqrt(HD)
    qlane = lax.broadcasted_iota(jnp.int32, (qblock, 128), 1)

    for i in range(NS * ROWS // qblock):
        lo = left[i * qblock : (i + 1) * qblock].astype(F32)
        hi = right[i * qblock : (i + 1) * qblock].astype(F32)
        query = jnp.where(
            qlane < 56, pltpu.roll(lo, 56, 1), jnp.where(qlane < HD, pltpu.roll(hi, 112, 1), 0.0)
        ).astype(BF)
        scores = lax.dot_general(query, left, (((1,), (1,)), ((), ())), preferred_element_type=F32)
        top = jnp.max(scores, axis=1, keepdims=True)
        probs = jnp.exp2((scores - top) * factor).astype(BF)
        mixed = jnp.dot(probs, values, preferred_element_type=F32)
        mixed = (mixed / mixed[:, HD : HD + 1]).astype(BF)
        each = qblock // ROWS
        att[pl.ds(i * each, each)] = mixed.reshape(each, ROWS, 128)
        for j in range(each):
            to = i * each + j

            @pl.when(s != to)
            def _():
                remote(att.at[to], attgot.at[s], att_s, att_r, f, to).start()

        if i == 1:
            relay(0, wp, 1)
    attgot[s] = att[s]

    relay(0, wp, 2)
    wt_more = begin(1, wtq, wt, wt_y, wt_c)
    ring_arrived(0, wp, 3).wait_recv()
    die(0, wp, 3).start()

    total(attgot, NS - 1, att_r).wait_recv()
    rows = jnp.concatenate([attgot[h, :, 0:HD] for h in ORDER], axis=1)
    for k in range(4):
        die_arrived(0, wp, k).wait_recv()
    projected = jnp.dot(rows, wp[...].reshape(D, D), preferred_element_type=F32)
    hidden = lat_ref[...].astype(F32) + gate_ref[...] * (projected + bias_ref[...])
    hidden_ref[...] = hidden
    mean = jnp.mean(hidden, axis=1, keepdims=True)
    centred = hidden - mean
    variance = jnp.mean(centred * centred, axis=1, keepdims=True)
    flat[...] = centred * lax.rsqrt(variance + 1e-06) * (1.0 + scale_ref[...]) + shift_ref[...]
    normed = jnp.concatenate([flat[:, pl.ds(h * HD, HD)] for h in ORDER], axis=1)
    for g in range(ROWS // GROUP):
        toks[g] = normed[g * GROUP : (g + 1) * GROUP].astype(BF)

    def send_tok(i, _):
        to = (f + i) % NF
        remote(toks.at[to % 16], tokgot.at[f], tok_s, tok_r, to, s).start()
        return 0

    lax.fori_loop(1, NF, send_tok, 0)
    tokgot[f] = toks[group]

    for k in range(3):
        relay(1, wt, k)
    ring_arrived(1, wt, 3).wait_recv()
    die(1, wt, 3).start()
    total(tokgot, NF - 1, tok_r).wait_recv()
    x = jnp.concatenate([tokgot[i].astype(F32) for i in range(NF)], axis=0).astype(BF)
    for k in range(4):
        die_arrived(1, wt, k).wait_recv()
    packed = jnp.dot(x, wt[...].reshape(D, WT), preferred_element_type=F32).astype(BF)
    allowed = mask_ref[...] > 0.5
    parts = []
    for h in range(HEADS // 2):
        qh = packed[:, h * HD : (h + 1) * HD]
        kh = packed[:, HALF + h * HD : HALF + (h + 1) * HD]
        vh = packed[:, 2 * HALF + h * HD : 2 * HALF + (h + 1) * HD]
        scores = lax.dot_general(qh, kh, (((1,), (1,)), ((), ())), preferred_element_type=F32)
        scores = jnp.where(allowed, scores * (1.0 / math.sqrt(HD)), NEG)
        top = jnp.max(scores, axis=1, keepdims=True)
        probs = jnp.exp(scores - top)
        whole = jnp.sum(probs, axis=1, keepdims=True)
        parts.append(jnp.dot(probs.astype(BF), vh, preferred_element_type=F32) / whole)
    mixed = jnp.concatenate(parts, axis=1)
    for i in range(NF):
        rets[i] = mixed[i * GROUP : (i + 1) * GROUP].astype(BF)

    def send_ret(i, _):
        to = (f + i) % NF
        remote(rets.at[to], retgot.at[f], ret_s, ret_r, to, s).start()
        return 0

    lax.fori_loop(1, NF, send_ret, 0)
    retgot[f] = rets[f]

    for copy in (wp_y, wp_c, wt_y, wt_c, wp_more, wt_more):
        copy.wait_send()
    for m, buf in ((0, wp), (1, wt)):
        for k in range(4):
            ring(m, buf, k).wait_send()
            die(m, buf, k).wait_send()
    total(pack, NS - 1, qkv_s).wait_send()
    total(att, NS - 1, att_s).wait_send()
    for i in range(2):
        n = 16 if i == 0 else 15
        remote(toks.at[pl.ds(0, n)], toks.at[pl.ds(0, n)], tok_s, tok_s, f, s).wait_send()
    total(rets, NF - 1, ret_s).wait_send()

    total(retgot, NF - 1, ret_r).wait_recv()
    out_ref[...] = retgot[...]


def shards(q, k, v, lat, wp, bias, gate, shift, scale, wt, clips):
    wt_halves = jnp.transpose(wt.reshape(SHARD, 3, 2, HALF), (2, 0, 1, 3)).reshape(2, SHARD, WT)
    flat2 = lambda a: a.reshape(ROWS, D)
    vec = lambda a: a.reshape(1, D)
    vmem = pl.BlockSpec(memory_space=pltpu.VMEM)
    hidden, got = pl.pallas_call(
        kernel,
        out_shape=(
            jax.ShapeDtypeStruct((ROWS, D), F32),
            jax.ShapeDtypeStruct((NF, GROUP, HALF), BF),
        ),
        in_specs=[pl.BlockSpec(memory_space=pltpu.SMEM)] + [vmem] * 10,
        out_specs=(vmem, vmem),
        scratch_shapes=[
            pltpu.VMEM((NS, ROWS, 256), BF),
            pltpu.VMEM((NS, ROWS, 256), BF),
            pltpu.VMEM((NS, ROWS, 128), BF),
            pltpu.VMEM((NS, ROWS, 128), BF),
            pltpu.VMEM((4, SHARD, D), BF),
            pltpu.VMEM((4, SHARD, WT), BF),
            pltpu.VMEM((NZ, QUAD, D), BF),
            pltpu.VMEM((NZ, QUAD, WT), BF),
            pltpu.VMEM((ROWS // GROUP, GROUP, D), BF),
            pltpu.VMEM((NF, GROUP, D), BF),
            pltpu.VMEM((NF, GROUP, HALF), BF),
            pltpu.VMEM((NF, GROUP, HALF), BF),
            pltpu.VMEM((ROWS, D), F32),
            pltpu.VMEM((TOK, TOK), F32),
        ]
        + [pltpu.SemaphoreType.DMA] * 8
        + [
            pltpu.SemaphoreType.DMA((6,)),
            pltpu.SemaphoreType.DMA((6,)),
            pltpu.SemaphoreType.DMA((8,)),
            pltpu.SemaphoreType.DMA((8,)),
            pltpu.SemaphoreType.DMA((8,)),
            pltpu.SemaphoreType.DMA((8,)),
        ],
        compiler_params=pltpu.CompilerParams(
            collective_id=0, has_side_effects=True, vmem_limit_bytes=56 * 1024 * 1024
        ),
        name="stdit",
    )(clips, flat2(q), flat2(k), flat2(v), flat2(lat), wp, wt_halves, vec(bias), vec(gate), vec(shift), vec(scale))
    temporal = jnp.transpose(got.reshape(2, 16, GROUP, HALF), (1, 2, 0, 3)).reshape(1, ROWS, D)
    return hidden.reshape(1, ROWS, D), temporal.astype(F32)


def solution(mesh):
    both = P("frame", "space", None)
    return jax.shard_map(
        shards,
        mesh=mesh,
        in_specs=(both, both, both, both, P("frame", None), P(), P(), P(), P(), P("frame", None), P()),
        out_specs=(both, both),
        check_vma=False,
    )
```

time: 207 us -> 108 us (0.52)
  Pallas kernels: 0 us -> 98.5 us
  waiting for transfers between devices: 97.6 us -> 0 us
  starting transfers between devices: 30.3 us -> 0 us
  local copies, waits for them, and re-layouts: 29.8 us -> 7.71 us
  blocking collectives: 21.3 us -> 0 us
  between operations: 14.4 us -> 0.69 us
  matrix products: 8.13 us -> 0 us
  other arithmetic: 4.11 us -> 0.94 us
    pallas_call x0 -> x1, Pallas kernels: none -> 98.5 us  [shards(): pl.pallas_call(kernel, out_shape=(jax.ShapeDtypeStruct((ROWS, D), F32), j...]
    all_gather x2 -> x0, waiting for transfers between devices: 49.2 us -> none  [the longest x1 49.2 us: shards(): whole_weight = lax.all_gather(temporal_weight, FRAME, axis=0, tiled=True)]
    all_to_all x5 -> x0, waiting for transfers between devices: 47 us -> none  [the longest x1 14.1 us: shards(): lax.all_to_all(spatial_value.reshape(split), 'space', split_axis=2, conca...]
    all_to_all x5 -> x0, starting transfers between devices: 30.2 us -> none  [the longest x1 10.2 us: shards(): lax.all_to_all(query, 'space', split_axis=2, concat_axis=1, tiled=True)]
    all_to_all x2 -> x0, blocking collectives: 21.3 us -> none  [the longest x1 14.6 us: shards(): lax.all_to_all(temporal.astype(jnp.bfloat16), FRAME, split_axis=0, concat...]
    unnamed x21 -> x9, local copies, waits for them, and re-layouts: 18.7 us -> 0.93 us
    dot_general x8 -> x0, matrix products: 8.13 us -> none  [the longest x1 4.58 us: shards(): jnp.einsum('fnc,ce->fne', exchange_by_chip(normed.reshape(frames_dev, gro...]
    unnamed x1 -> x0, other arithmetic: 2.27 us -> none
  transfers between devices with their start and end apart: 7 -> 0, of which waited for: 5 -> 0; matrix products, arithmetic and copies ran while one was open for 16% -> 0% of each run, Pallas kernels for 0% -> 0%
where the time goes in v1:
time: 108 us
  Pallas kernels  98.5 us (91%)
  local copies, waits for them, and re-layouts  7.71 us (7%)
    pallas_call x1, Pallas kernels, shards(): pl.pallas_call(kernel, out_shape=(jax.ShapeDtypeStruct((ROWS, D), F32), j...  98.5 us
    reshape x4, local copies, waits for them, and re-layouts, shards(): vec = lambda a: a.reshape(1, D)  3.08 us

profile of v1, /device:TPU:1, one launch (start us, length us, event | category | flops | bytes accessed | tf_op | source)
XLA Modules:
  0.0 107.9 jit_solution(10976261530559565667)
XLA Ops:
  0.6 0.0 copy-start.1
  0.6 1.3 %reshape.61.bias_ref = f32[1,1152]{1,0:T(1,128)} reshape(f32[1152]{0:T(1024)} %param.16) | data formatting | bytes 9216 | tf_op jit(solution)/shard_map/reshape | solution.py:272
  1.9 0.0 copy-done.1
  1.9 0.0 copy-start.2
  1.9 0.6 reshape.62.gate_ref
  2.5 0.1 copy-done.2
  2.6 0.0 copy-start.3
  2.6 0.6 reshape.63.shift_ref
  3.2 0.1 copy-done.3
  3.3 0.6 reshape.64.scale_ref
  3.9 1.2 %reshape.59 = bf16[36,3,2,576]{3,2,1,0:T(2,128)(2,1)S(1)} reshape(bf16[36,3456]{1,0:T(8,128)(2,1)} %param.20) | data formatting | bytes 497664 | tf_op jit(solution)/shard_map/reshape | solution.py:270
  5.1 0.1 copy.19
  5.3 0.4 reshape.60
  5.7 0.7 copy.16.wt_ref
  6.4 98.5 %stdit.1 = (f32[64,1152]{1,0:T(8,128)}, bf16[32,4,576]{2,1,0:T(4,128)(2,1)}) custom-call(s32[16]{0:T(128)} %clip_ref.1, bf16[64,1152]{1,0:T(8,128)(2,1)} %bitcast.17, bf16[64,1152]{1,0:T(8,128)(2,1)} %bitcast.18, bf16[64,1152]{1,0:T(8,128)(2,1)} %bitcast.19, bf16[64,1152]{1,0:T(8,128)(2,1)} %bitcast.20, bf16[36,1152]{1,0:T(8,128)(2,1)} %wp_ref.1, ...), custom_call_target="tpu_custom_call" | custom-call | tf_op jit(solution)/shard_map/stdit/pallas_call | solution.py:274
  105.0 0.9 convert_bitcast_fusion
  105.9 0.3 copy.17
  106.2 0.0 copy-start
  106.2 1.0 reshape.66
  107.1 0.0 copy-done
  107.1 0.7 copy.21
Async XLA Ops:
  0.6 1.3 %copy-start.1 = (f32[1152]{0:T(1024)S(1)}, f32[1152]{0:T(1024)}, u32[]{:S(2)}) copy-start(f32[1152]{0:T(1024)} %param.17) | copy-start | bytes 13828
  1.9 0.7 copy-start.2
  2.6 0.7 copy-start.3
  106.2 1.0 copy-start

commit v2 on v1

--- a/solution.py
+++ b/solution.py
@@ -26,6 +26,11 @@
 TOK = NF * GROUP
 NEG = -1e30
 LOG2E = 1.4426950408889634
+CHUNKS = (
+    ((0, 384), (384, 384), (768, 384)),
+    ((0, 640), (640, 640), (1280, 448)),
+)
+NC = 3
 
 ORDER = tuple((j % 2) * 8 + j // 2 for j in range(HEADS))
 
@@ -39,7 +44,7 @@
 def kernel(
     clip_ref, q_ref, k_ref, v_ref, lat_ref, wp_ref, wt_ref, bias_ref, gate_ref, shift_ref, scale_ref,
     hidden_ref, out_ref,
-    pack, got, att, attgot, wpq, wtq, wp, wt, toks, tokgot, rets, retgot, flat, mask_ref,
+    pack, got, att, attgot, wpq, wtq, wp, wt, toks, tokgot, rets, retgot, flat, mask_ref, wto,
     qkv_s, qkv_r, att_s, att_r, tok_s, tok_r, ret_s, ret_r,
     pre_s, pre_r, ring_s, ring_r, die_s, die_r,
 ):
@@ -78,7 +83,14 @@
         pack[h, :, 0:128] = jnp.concatenate([kk, qq[:, :56]], axis=1)
         pack[h, :, 128:256] = jnp.concatenate([vv, qq[:, 56:], jnp.zeros((ROWS, 40), BF)], axis=1)
     wpq[me_q] = wp_ref[...]
-    wtq[me_q] = wt_ref[row]
+    for r in range(2):
+
+        @pl.when(row == r)
+        def _():
+            mine = [wt_ref[:, pl.ds(t * D + r * HALF, HALF)] for t in range(3)]
+            rest = [wt_ref[:, pl.ds(t * D + (1 - r) * HALF, HALF)] for t in range(3)]
+            wtq[me_q] = jnp.concatenate(mine, axis=1)
+            wto[...] = jnp.concatenate(rest, axis=1)
 
     pl.semaphore_wait(barrier, NS - 1 + NF - 1 + 1)
 
@@ -93,37 +105,45 @@
         return 0
 
     lax.fori_loop(1, NS, send_qkv, 0)
-    wt_y = remote(wt_ref.at[1 - row], wtq.at[me_q], pre_s.at[2], pre_r.at[2], other, s)
-    wt_c = remote(wt_ref.at[row], wtq.at[me_q], pre_s.at[3], pre_r.at[3], sib, s)
+    wt_y = remote(wto, wtq.at[me_q], pre_s.at[2], pre_r.at[2], other, s)
+    wt_c = remote(wtq.at[me_q], wtq.at[me_q], pre_s.at[3], pre_r.at[3], sib, s)
     wt_y.start()
     wt_c.start()
     got[s] = pack[s]
 
-    def ring(m, buf, k):
-        block = (z - step * k + 2 * NZ) % NZ
-        src = buf.at[block] if k < 3 else buf.at[block, pl.ds(pl.multiple_of(c * 64, 16), 80)]
-        return remote(src, src, ring_s.at[m * 4 + k], ring_r.at[m * 4 + k], fz, s)
-
-    def ring_arrived(m, buf, k):
-        block = (z - step * (k + 1) + 2 * NZ) % NZ
-        dst = buf.at[block] if k < 3 else buf.at[block, pl.ds(pl.multiple_of(c * 64, 16), 80)]
-        return remote(dst, dst, ring_s.at[m * 4 + k], ring_r.at[m * 4 + k], fz, s)
-
-    def die(m, buf, k):
-        block = (z - step * (k + 1) + 2 * NZ) % NZ
-        src = buf.at[block] if k < 3 else buf.at[block, pl.ds(pl.multiple_of(c * 80, 16), 64)]
-        return remote(src, src, die_s.at[m * 4 + k], die_r.at[m * 4 + k], sib, s)
-
-    def die_arrived(m, buf, k):
-        block = (z + step * (k + 1) + 2 * NZ) % NZ
-        dst = buf.at[block] if k < 3 else buf.at[block, pl.ds(pl.multiple_of((1 - c) * 80, 16), 64)]
-        return remote(dst, dst, die_s.at[m * 4 + k], die_r.at[m * 4 + k], sib, s)
-
-    def relay(m, buf, k):
-        ring_arrived(m, buf, k).wait_recv()
+    def piece(m, buf, block, k, first, rows, n):
+        cut = pl.ds(*CHUNKS[m][n])
+        block = (block + 2 * NZ) % NZ
         if k < 3:
-            ring(m, buf, k + 1).start()
-        die(m, buf, k).start()
+            return buf.at[block, :, cut]
+        return buf.at[block, pl.ds(pl.multiple_of(first, 16), rows), cut]
+
+    def ring(m, buf, k, n):
+        src = piece(m, buf, z - step * k, k, c * 64, 80, n)
+        at = (m * 4 + k) * NC + n
+        return remote(src, src, ring_s.at[at], ring_r.at[at], fz, s)
+
+    def ring_arrived(m, buf, k, n):
+        dst = piece(m, buf, z - step * (k + 1), k, c * 64, 80, n)
+        at = (m * 4 + k) * NC + n
+        return remote(dst, dst, ring_s.at[at], ring_r.at[at], fz, s)
+
+    def die(m, buf, k, n):
+        src = piece(m, buf, z - step * (k + 1), k, c * 80, 64, n)
+        at = (m * 4 + k) * NC + n
+        return remote(src, src, die_s.at[at], die_r.at[at], sib, s)
+
+    def die_arrived(m, buf, k, n):
+        dst = piece(m, buf, z + step * (k + 1), k, (1 - c) * 80, 64, n)
+        at = (m * 4 + k) * NC + n
+        return remote(dst, dst, die_s.at[at], die_r.at[at], sib, s)
+
+    def relay(m, buf, k, chunks=range(NC)):
+        for n in chunks:
+            ring_arrived(m, buf, k, n).wait_recv()
+            if k < 3:
+                ring(m, buf, k + 1, n).start()
+            die(m, buf, k, n).start()
 
     def begin(m, quads, buf, over_y, over_c):
         over_y.wait_recv()
@@ -132,7 +152,8 @@
         over_c.wait_recv()
         more.wait_recv()
         buf[z] = jnp.concatenate([quads[i].astype(F32) for i in range(4)], axis=0).astype(BF)
-        ring(m, buf, 0).start()
+        for n in range(NC):
+            ring(m, buf, 0, n).start()
         return more
 
     wp_more = begin(0, wpq, wp, wp_y, wp_c)
@@ -150,6 +171,7 @@
     mask_ref[...] = jnp.where(same, 1.0, 0.0)
 
     relay(0, wp, 0)
+    relay(0, wp, 1)
 
     def total(buf, n, recv):
         return remote(buf.at[pl.ds(0, n)], buf.at[pl.ds(0, n)], recv, recv, f, s)
@@ -184,19 +206,21 @@
             def _():
                 remote(att.at[to], attgot.at[s], att_s, att_r, f, to).start()
 
+        if i == 0:
+            relay(0, wp, 2)
         if i == 1:
-            relay(0, wp, 1)
+            relay(0, wp, 3)
+            wt_more = begin(1, wtq, wt, wt_y, wt_c)
+        if i == 3:
+            relay(1, wt, 0)
     attgot[s] = att[s]
-
-    relay(0, wp, 2)
-    wt_more = begin(1, wtq, wt, wt_y, wt_c)
-    ring_arrived(0, wp, 3).wait_recv()
-    die(0, wp, 3).start()
 
     total(attgot, NS - 1, att_r).wait_recv()
     rows = jnp.concatenate([attgot[h, :, 0:HD] for h in ORDER], axis=1)
     for k in range(4):
-        die_arrived(0, wp, k).wait_recv()
+        for n in range(NC):
+            die_arrived(0, wp, k, n).wait_recv()
+    relay(1, wt, 1)
     projected = jnp.dot(rows, wp[...].reshape(D, D), preferred_element_type=F32)
     hidden = lat_ref[...].astype(F32) + gate_ref[...] * (projected + bias_ref[...])
     hidden_ref[...] = hidden
@@ -216,14 +240,13 @@
     lax.fori_loop(1, NF, send_tok, 0)
     tokgot[f] = toks[group]
 
-    for k in range(3):
-        relay(1, wt, k)
-    ring_arrived(1, wt, 3).wait_recv()
-    die(1, wt, 3).start()
+    relay(1, wt, 2)
+    relay(1, wt, 3)
     total(tokgot, NF - 1, tok_r).wait_recv()
     x = jnp.concatenate([tokgot[i].astype(F32) for i in range(NF)], axis=0).astype(BF)
     for k in range(4):
-        die_arrived(1, wt, k).wait_recv()
+        for n in range(NC):
+            die_arrived(1, wt, k, n).wait_recv()
     packed = jnp.dot(x, wt[...].reshape(D, WT), preferred_element_type=F32).astype(BF)
     allowed = mask_ref[...] > 0.5
     parts = []
@@ -253,8 +276,9 @@
         copy.wait_send()
     for m, buf in ((0, wp), (1, wt)):
         for k in range(4):
-            ring(m, buf, k).wait_send()
-            die(m, buf, k).wait_send()
+            for n in range(NC):
+                ring(m, buf, k, n).wait_send()
+                die(m, buf, k, n).wait_send()
     total(pack, NS - 1, qkv_s).wait_send()
     total(att, NS - 1, att_s).wait_send()
     for i in range(2):
@@ -263,19 +287,19 @@
     total(rets, NF - 1, ret_s).wait_send()
 
     total(retgot, NF - 1, ret_r).wait_recv()
-    out_ref[...] = retgot[...]
+    for g in range(0, 16, 2):
+        pair = [jnp.concatenate([retgot[i].astype(F32), retgot[16 + i].astype(F32)], axis=1) for i in (g, g + 1)]
+        out_ref[pl.ds(g * GROUP, 2 * GROUP), :] = jnp.concatenate(pair, axis=0)
 
 
 def shards(q, k, v, lat, wp, bias, gate, shift, scale, wt, clips):
-    wt_halves = jnp.transpose(wt.reshape(SHARD, 3, 2, HALF), (2, 0, 1, 3)).reshape(2, SHARD, WT)
     flat2 = lambda a: a.reshape(ROWS, D)
-    vec = lambda a: a.reshape(1, D)
     vmem = pl.BlockSpec(memory_space=pltpu.VMEM)
-    hidden, got = pl.pallas_call(
+    hidden, temporal = pl.pallas_call(
         kernel,
         out_shape=(
             jax.ShapeDtypeStruct((ROWS, D), F32),
-            jax.ShapeDtypeStruct((NF, GROUP, HALF), BF),
+            jax.ShapeDtypeStruct((ROWS, D), F32),
         ),
         in_specs=[pl.BlockSpec(memory_space=pltpu.SMEM)] + [vmem] * 10,
         out_specs=(vmem, vmem),
@@ -294,23 +318,23 @@
             pltpu.VMEM((NF, GROUP, HALF), BF),
             pltpu.VMEM((ROWS, D), F32),
             pltpu.VMEM((TOK, TOK), F32),
+            pltpu.VMEM((SHARD, WT), BF),
         ]
         + [pltpu.SemaphoreType.DMA] * 8
         + [
             pltpu.SemaphoreType.DMA((6,)),
             pltpu.SemaphoreType.DMA((6,)),
-            pltpu.SemaphoreType.DMA((8,)),
-            pltpu.SemaphoreType.DMA((8,)),
-            pltpu.SemaphoreType.DMA((8,)),
-            pltpu.SemaphoreType.DMA((8,)),
+            pltpu.SemaphoreType.DMA((8 * NC,)),
+            pltpu.SemaphoreType.DMA((8 * NC,)),
+            pltpu.SemaphoreType.DMA((8 * NC,)),
+            pltpu.SemaphoreType.DMA((8 * NC,)),
         ],
         compiler_params=pltpu.CompilerParams(
             collective_id=0, has_side_effects=True, vmem_limit_bytes=56 * 1024 * 1024
         ),
         name="stdit",
-    )(clips, flat2(q), flat2(k), flat2(v), flat2(lat), wp, wt_halves, vec(bias), vec(gate), vec(shift), vec(scale))
-    temporal = jnp.transpose(got.reshape(2, 16, GROUP, HALF), (1, 2, 0, 3)).reshape(1, ROWS, D)
-    return hidden.reshape(1, ROWS, D), temporal.astype(F32)
+    )(clips, flat2(q), flat2(k), flat2(v), flat2(lat), wp, wt, bias, gate, shift, scale)
+    return hidden.reshape(1, ROWS, D), temporal.reshape(1, ROWS, D)
 
 
 def solution(mesh):

time: 108 us -> 94.4 us (0.87)
  Pallas kernels: 98.5 us -> 91.1 us
  local copies, waits for them, and re-layouts: 7.71 us -> 2.46 us
    pallas_call x1, Pallas kernels: 98.5 us -> 91.1 us  [shards(): pl.pallas_call(kernel, out_shape=(jax.ShapeDtypeStruct((ROWS, D), F32), j...]
    reshape x8 -> x0, local copies, waits for them, and re-layouts: 5.55 us -> none  [the longest x4 3.08 us: shards(): vec = lambda a: a.reshape(1, D)]
    unnamed x9 -> x4, local copies, waits for them, and re-layouts: 0.93 us -> 2.46 us
    convert_element_type x2 -> x0, local copies, waits for them, and re-layouts: 1.23 us -> none  [shards(): return (hidden.reshape(1, ROWS, D), temporal.astype(F32))]
where the time goes in v2:
time: 94.4 us; the launch traced here: 94.2 us
  Pallas kernels  91.1 us (97%)
  local copies, waits for them, and re-layouts  2.46 us (3%)
    pallas_call x1, Pallas kernels, shards(): pl.pallas_call(kernel, out_shape=(jax.ShapeDtypeStruct((ROWS, D), F32), j...  91.1 us
    unnamed x4, local copies, waits for them, and re-layouts  2.46 us

profile of v2, /device:TPU:1, one launch (start us, length us, event | category | flops | bytes accessed | tf_op | source)
XLA Modules:
  0.0 94.2 jit_solution(12691905401796213455)
XLA Ops:
  0.6 91.1 %stdit.1 = (f32[64,1152]{1,0:T(8,128)}, f32[64,1152]{1,0:T(8,128)}) custom-call(s32[16]{0:T(128)} %clip_ref.1, bf16[64,1152]{1,0:T(8,128)(2,1)} %bitcast.8, bf16[64,1152]{1,0:T(8,128)(2,1)} %bitcast.9, bf16[64,1152]{1,0:T(8,128)(2,1)} %bitcast.10, bf16[64,1152]{1,0:T(8,128)(2,1)} %bitcast.11, bf16[36,1152]{1,0:T(8,128)(2,1)} %wp_ref.1, ...), custom_call_target="tpu_custom_call" | custom-call | tf_op jit(solution)/shard_map/stdit/pallas_call | solution.py:298
  91.7 0.0 copy-start
  91.8 1.7 %copy.15 = f32[1,64,1152]{2,1,0:T(8,128)} copy(f32[1,64,1152]{2,1,0:T(8,128)} %bitcast.7) | data formatting | bytes 589824
  93.5 0.0 copy-done
  93.5 0.7 copy.16
Async XLA Ops:
  91.7 1.8 %copy-start = (f32[64,1152]{1,0:T(8,128)S(1)}, f32[64,1152]{1,0:T(8,128)}, u32[]{:S(2)}) copy-start(f32[64,1152]{1,0:T(8,128)} %get-tuple-element.5) | copy-start | bytes 884740

commit v3 on v2

--- a/solution.py
+++ b/solution.py
@@ -26,10 +26,8 @@
 TOK = NF * GROUP
 NEG = -1e30
 LOG2E = 1.4426950408889634
-CHUNKS = (
-    ((0, 384), (384, 384), (768, 384)),
-    ((0, 640), (640, 640), (1280, 448)),
-)
+SHARED = ((0, 384), (1024, 704))
+SWAPPED = ((384, 384), (0, 512))
 NC = 3
 
 ORDER = tuple((j % 2) * 8 + j // 2 for j in range(HEADS))
@@ -46,7 +44,7 @@
     hidden_ref, out_ref,
     pack, got, att, attgot, wpq, wtq, wp, wt, toks, tokgot, rets, retgot, flat, mask_ref, wto,
     qkv_s, qkv_r, att_s, att_r, tok_s, tok_r, ret_s, ret_r,
-    pre_s, pre_r, ring_s, ring_r, die_s, die_r,
+    pre_s, pre_r, ring_s, ring_r, die_s, die_r, swap_s, swap_r,
 ):
     f = lax.axis_index("frame")
     s = lax.axis_index("space")
@@ -62,6 +60,9 @@
     sb = (s - yhi) + (yhi + 2 * row - 1 + 4) % 4
     me_q = row * 2 + c
     other_q = (1 - row) * 2 + c
+    x = s // 4
+    part = (x % 2, x // 2)
+    beside = (s + 4 * (1 - 2 * (x % 2)), (3 - x) * 4 + yhi)
 
     barrier = pltpu.get_barrier_semaphore()
 
@@ -98,21 +99,26 @@
     wp_c = remote(wp_ref, wpq.at[me_q], pre_s.at[1], pre_r.at[1], sib, s)
     wp_y.start()
     wp_c.start()
-
-    def send_qkv(i, _):
-        to = (s + i) % NS
-        remote(pack.at[to], got.at[s], qkv_s, qkv_r, f, to).start()
-        return 0
-
-    lax.fori_loop(1, NS, send_qkv, 0)
     wt_y = remote(wto, wtq.at[me_q], pre_s.at[2], pre_r.at[2], other, s)
     wt_c = remote(wtq.at[me_q], wtq.at[me_q], pre_s.at[3], pre_r.at[3], sib, s)
     wt_y.start()
     wt_c.start()
+
+    def send_qkv(i, _):
+        to = (s + i) % NS
+        remote(pack.at[to], got.at[s], qkv_s, qkv_r, f, to).start()
+        return 0
+
+    lax.fori_loop(1, NS, send_qkv, 0)
     got[s] = pack[s]
 
     def piece(m, buf, block, k, first, rows, n):
-        cut = pl.ds(*CHUNKS[m][n])
+        if n == 0:
+            cut = pl.ds(*SHARED[m])
+        else:
+            first_column, width = SWAPPED[m]
+            which = part[m] if n == 1 else 1 - part[m]
+            cut = pl.ds(pl.multiple_of(first_column + which * width, 128), width)
         block = (block + 2 * NZ) % NZ
         if k < 3:
             return buf.at[block, :, cut]
@@ -138,12 +144,22 @@
         at = (m * 4 + k) * NC + n
         return remote(dst, dst, die_s.at[at], die_r.at[at], sib, s)
 
-    def relay(m, buf, k, chunks=range(NC)):
+    def swap(m, buf, k, n):
+        ref = piece(m, buf, z - step * (k + 1), k, c * 64, 80, n)
+        return remote(ref, ref, swap_s.at[m * 4 + k], swap_r.at[m * 4 + k], f, beside[m])
+
+    def relay(m, buf, k, chunks=(0, 1)):
         for n in chunks:
             ring_arrived(m, buf, k, n).wait_recv()
             if k < 3:
                 ring(m, buf, k + 1, n).start()
+            if n == 1:
+                swap(m, buf, k, 1).start()
             die(m, buf, k, n).start()
+
+    def swapped(m, buf, k):
+        swap(m, buf, k, 2).wait_recv()
+        die(m, buf, k, 2).start()
 
     def begin(m, quads, buf, over_y, over_c):
         over_y.wait_recv()
@@ -152,11 +168,12 @@
         over_c.wait_recv()
         more.wait_recv()
         buf[z] = jnp.concatenate([quads[i].astype(F32) for i in range(4)], axis=0).astype(BF)
-        for n in range(NC):
+        for n in range(2 - m):
             ring(m, buf, 0, n).start()
         return more
 
     wp_more = begin(0, wpq, wp, wp_y, wp_c)
+    wt_more = begin(1, wtq, wt, wt_y, wt_c)
 
     ri = lax.broadcasted_iota(jnp.int32, (TOK, TOK), 0)
     ci = lax.broadcasted_iota(jnp.int32, (TOK, TOK), 1)
@@ -171,7 +188,7 @@
     mask_ref[...] = jnp.where(same, 1.0, 0.0)
 
     relay(0, wp, 0)
-    relay(0, wp, 1)
+    ring(1, wt, 0, 1).start()
 
     def total(buf, n, recv):
         return remote(buf.at[pl.ds(0, n)], buf.at[pl.ds(0, n)], recv, recv, f, s)
@@ -206,22 +223,29 @@
             def _():
                 remote(att.at[to], attgot.at[s], att_s, att_r, f, to).start()
 
-        if i == 0:
-            relay(0, wp, 2)
         if i == 1:
-            relay(0, wp, 3)
-            wt_more = begin(1, wtq, wt, wt_y, wt_c)
+            relay(0, wp, 1)
         if i == 3:
-            relay(1, wt, 0)
+            relay(1, wt, 0, (0,))
     attgot[s] = att[s]
+
+    swapped(0, wp, 0)
+    relay(0, wp, 2)
+    relay(1, wt, 0, (1,))
+    swapped(0, wp, 1)
+    relay(0, wp, 3)
+    relay(1, wt, 1, (0,))
+    swapped(0, wp, 2)
+    relay(1, wt, 1, (1,))
+    swapped(0, wp, 3)
 
     total(attgot, NS - 1, att_r).wait_recv()
     rows = jnp.concatenate([attgot[h, :, 0:HD] for h in ORDER], axis=1)
     for k in range(4):
         for n in range(NC):
             die_arrived(0, wp, k, n).wait_recv()
-    relay(1, wt, 1)
     projected = jnp.dot(rows, wp[...].reshape(D, D), preferred_element_type=F32)
+    relay(1, wt, 2, (0,))
     hidden = lat_ref[...].astype(F32) + gate_ref[...] * (projected + bias_ref[...])
     hidden_ref[...] = hidden
     mean = jnp.mean(hidden, axis=1, keepdims=True)
@@ -240,14 +264,18 @@
     lax.fori_loop(1, NF, send_tok, 0)
     tokgot[f] = toks[group]
 
-    relay(1, wt, 2)
+    relay(1, wt, 2, (1,))
+    swapped(1, wt, 0)
+    swapped(1, wt, 1)
     relay(1, wt, 3)
+    swapped(1, wt, 2)
+    swapped(1, wt, 3)
     total(tokgot, NF - 1, tok_r).wait_recv()
-    x = jnp.concatenate([tokgot[i].astype(F32) for i in range(NF)], axis=0).astype(BF)
+    tokens = jnp.concatenate([tokgot[i].astype(F32) for i in range(NF)], axis=0).astype(BF)
     for k in range(4):
         for n in range(NC):
             die_arrived(1, wt, k, n).wait_recv()
-    packed = jnp.dot(x, wt[...].reshape(D, WT), preferred_element_type=F32).astype(BF)
+    packed = jnp.dot(tokens, wt[...].reshape(D, WT), preferred_element_type=F32).astype(BF)
     allowed = mask_ref[...] > 0.5
     parts = []
     for h in range(HEADS // 2):
@@ -277,8 +305,10 @@
     for m, buf in ((0, wp), (1, wt)):
         for k in range(4):
             for n in range(NC):
-                ring(m, buf, k, n).wait_send()
+                if n < 2:
+                    ring(m, buf, k, n).wait_send()
                 die(m, buf, k, n).wait_send()
+            swap(m, buf, k, 1).wait_send()
     total(pack, NS - 1, qkv_s).wait_send()
     total(att, NS - 1, att_s).wait_send()
     for i in range(2):
@@ -328,6 +358,8 @@
             pltpu.SemaphoreType.DMA((8 * NC,)),
             pltpu.SemaphoreType.DMA((8 * NC,)),
             pltpu.SemaphoreType.DMA((8 * NC,)),
+            pltpu.SemaphoreType.DMA((8,)),
+            pltpu.SemaphoreType.DMA((8,)),
         ],
         compiler_params=pltpu.CompilerParams(
             collective_id=0, has_side_effects=True, vmem_limit_bytes=56 * 1024 * 1024

time: 94.4 us -> 81.1 us (0.86)
  Pallas kernels: 91.1 us -> 77.8 us
    pallas_call x1, Pallas kernels: 91.1 us -> 77.8 us  [shards(): pl.pallas_call(kernel, out_shape=(jax.ShapeDtypeStruct((ROWS, D), F32), j...]
where the time goes in v3:
time: 81.1 us; the launch traced here: 80.9 us
  Pallas kernels  77.8 us (96%)
  local copies, waits for them, and re-layouts  2.46 us (3%)
    pallas_call x1, Pallas kernels, shards(): pl.pallas_call(kernel, out_shape=(jax.ShapeDtypeStruct((ROWS, D), F32), j...  77.8 us
    unnamed x4, local copies, waits for them, and re-layouts  2.46 us

profile of v3, /device:TPU:1, one launch (start us, length us, event | category | flops | bytes accessed | tf_op | source)
XLA Modules:
  0.0 80.9 jit_solution(14282865030699987648)
XLA Ops:
  0.6 77.8 %stdit.1 = (f32[64,1152]{1,0:T(8,128)}, f32[64,1152]{1,0:T(8,128)}) custom-call(s32[16]{0:T(128)} %clip_ref.1, bf16[64,1152]{1,0:T(8,128)(2,1)} %bitcast.8, bf16[64,1152]{1,0:T(8,128)(2,1)} %bitcast.9, bf16[64,1152]{1,0:T(8,128)(2,1)} %bitcast.10, bf16[64,1152]{1,0:T(8,128)(2,1)} %bitcast.11, bf16[36,1152]{1,0:T(8,128)(2,1)} %wp_ref.1, ...), custom_call_target="tpu_custom_call" | custom-call | tf_op jit(solution)/shard_map/stdit/pallas_call | solution.py:328
  78.5 0.0 copy-start
  78.5 1.7 %copy.15 = f32[1,64,1152]{2,1,0:T(8,128)} copy(f32[1,64,1152]{2,1,0:T(8,128)} %bitcast.7) | data formatting | bytes 589824
  80.2 0.0 copy-done
  80.2 0.7 copy.16
Async XLA Ops:
  78.5 1.8 %copy-start = (f32[64,1152]{1,0:T(8,128)S(1)}, f32[64,1152]{1,0:T(8,128)}, u32[]{:S(2)}) copy-start(f32[64,1152]{1,0:T(8,128)} %get-tuple-element.5) | copy-start | bytes 884740

commit v4 on v3

--- a/solution.py
+++ b/solution.py
@@ -26,9 +26,12 @@
 TOK = NF * GROUP
 NEG = -1e30
 LOG2E = 1.4426950408889634
-SHARED = ((0, 384), (1024, 704))
-SWAPPED = ((384, 384), (0, 512))
-NC = 3
+WIDE = 14 * 128
+RINGED = ((512, 640), (896, 896))
+SWAPPED = ((640, 512), (896, 896))
+PIECES = (((0, 256), (256, 384)), ((0, 512), (512, 384)))
+NC = 2
+NP = 2
 
 ORDER = tuple((j % 2) * 8 + j // 2 for j in range(HEADS))
 
@@ -40,8 +43,9 @@
 
 
 def kernel(
-    clip_ref, q_ref, k_ref, v_ref, lat_ref, wp_ref, wt_ref, bias_ref, gate_ref, shift_ref, scale_ref,
-    hidden_ref, out_ref,
+    clip_ref, q_in, k_in, v_in, lat_in, wp_in, wt_in, bias_ref, gate_ref, shift_ref, scale_ref,
+    hidden_out, temporal_out,
+    q_ref, k_ref, v_ref, lat_ref, wp_ref, wt_ref, hidden_ref, out_ref, local,
     pack, got, att, attgot, wpq, wtq, wp, wt, toks, tokgot, rets, retgot, flat, mask_ref, wto,
     qkv_s, qkv_r, att_s, att_r, tok_s, tok_r, ret_s, ret_r,
     pre_s, pre_r, ring_s, ring_r, die_s, die_r, swap_s, swap_r,
@@ -64,6 +68,15 @@
     part = (x % 2, x // 2)
     beside = (s + 4 * (1 - 2 * (x % 2)), (3 - x) * 4 + yhi)
 
+    loads = [
+        pltpu.make_async_copy(src, dst, local.at[i])
+        for i, (src, dst) in enumerate(
+            ((wp_in, wp_ref), (wt_in, wt_ref), (k_in, k_ref), (q_in, q_ref), (v_in, v_ref), (lat_in, lat_ref))
+        )
+    ]
+    for load in loads:
+        load.start()
+
     barrier = pltpu.get_barrier_semaphore()
 
     def hail_space(i, _):
@@ -78,6 +91,8 @@
     lax.fori_loop(1, NF, hail_frame, 0)
     pl.semaphore_signal(barrier, inc=1, device_id=(other, sb), device_id_type=MESH)
 
+    for load in loads:
+        load.wait()
     for h in range(HEADS):
         cut = pl.ds(h * HD, HD)
         kk, qq, vv = k_ref[:, cut], q_ref[:, cut], v_ref[:, cut]
@@ -90,8 +105,9 @@
         def _():
             mine = [wt_ref[:, pl.ds(t * D + r * HALF, HALF)] for t in range(3)]
             rest = [wt_ref[:, pl.ds(t * D + (1 - r) * HALF, HALF)] for t in range(3)]
-            wtq[me_q] = jnp.concatenate(mine, axis=1)
-            wto[...] = jnp.concatenate(rest, axis=1)
+            pad = [jnp.zeros((SHARD, WIDE - WT), BF)]
+            wtq[me_q] = jnp.concatenate(mine + pad, axis=1)
+            wto[...] = jnp.concatenate(rest + pad, axis=1)
 
     pl.semaphore_wait(barrier, NS - 1 + NF - 1 + 1)
 
@@ -112,54 +128,50 @@
     lax.fori_loop(1, NS, send_qkv, 0)
     got[s] = pack[s]
 
-    def piece(m, buf, block, k, first, rows, n):
-        if n == 0:
-            cut = pl.ds(*SHARED[m])
-        else:
-            first_column, width = SWAPPED[m]
-            which = part[m] if n == 1 else 1 - part[m]
-            cut = pl.ds(pl.multiple_of(first_column + which * width, 128), width)
+    def piece(m, buf, block, k, first, rows, kind, own, skip=0, width=None):
+        apart, whole = kind[m]
+        which = part[m] if own else 1 - part[m]
+        cut = pl.ds(pl.multiple_of(which * apart + skip, 128), width or whole)
         block = (block + 2 * NZ) % NZ
         if k < 3:
             return buf.at[block, :, cut]
         return buf.at[block, pl.ds(pl.multiple_of(first, 16), rows), cut]
 
-    def ring(m, buf, k, n):
-        src = piece(m, buf, z - step * k, k, c * 64, 80, n)
-        at = (m * 4 + k) * NC + n
+    def ring(m, buf, k, i):
+        src = piece(m, buf, z - step * k, k, c * 64, 80, RINGED, True, *PIECES[m][i])
+        at = (m * 4 + k) * NP + i
         return remote(src, src, ring_s.at[at], ring_r.at[at], fz, s)
 
-    def ring_arrived(m, buf, k, n):
-        dst = piece(m, buf, z - step * (k + 1), k, c * 64, 80, n)
-        at = (m * 4 + k) * NC + n
+    def ring_arrived(m, buf, k, i):
+        dst = piece(m, buf, z - step * (k + 1), k, c * 64, 80, RINGED, True, *PIECES[m][i])
+        at = (m * 4 + k) * NP + i
         return remote(dst, dst, ring_s.at[at], ring_r.at[at], fz, s)
 
     def die(m, buf, k, n):
-        src = piece(m, buf, z - step * (k + 1), k, c * 80, 64, n)
+        src = piece(m, buf, z - step * (k + 1), k, c * 80, 64, *((RINGED, True) if n == 0 else (SWAPPED, False)))
         at = (m * 4 + k) * NC + n
         return remote(src, src, die_s.at[at], die_r.at[at], sib, s)
 
     def die_arrived(m, buf, k, n):
-        dst = piece(m, buf, z + step * (k + 1), k, (1 - c) * 80, 64, n)
+        dst = piece(m, buf, z + step * (k + 1), k, (1 - c) * 80, 64, *((RINGED, True) if n == 0 else (SWAPPED, False)))
         at = (m * 4 + k) * NC + n
         return remote(dst, dst, die_s.at[at], die_r.at[at], sib, s)
 
     def swap(m, buf, k, n):
-        ref = piece(m, buf, z - step * (k + 1), k, c * 64, 80, n)
+        ref = piece(m, buf, z - step * (k + 1), k, c * 64, 80, SWAPPED, n == 1)
         return remote(ref, ref, swap_s.at[m * 4 + k], swap_r.at[m * 4 + k], f, beside[m])
 
-    def relay(m, buf, k, chunks=(0, 1)):
-        for n in chunks:
-            ring_arrived(m, buf, k, n).wait_recv()
+    def relay(m, buf, k):
+        for i in range(NP):
+            ring_arrived(m, buf, k, i).wait_recv()
             if k < 3:
-                ring(m, buf, k + 1, n).start()
-            if n == 1:
-                swap(m, buf, k, 1).start()
-            die(m, buf, k, n).start()
+                ring(m, buf, k + 1, i).start()
+        swap(m, buf, k, 1).start()
+        die(m, buf, k, 0).start()
 
     def swapped(m, buf, k):
         swap(m, buf, k, 2).wait_recv()
-        die(m, buf, k, 2).start()
+        die(m, buf, k, 1).start()
 
     def begin(m, quads, buf, over_y, over_c):
         over_y.wait_recv()
@@ -168,12 +180,11 @@
         over_c.wait_recv()
         more.wait_recv()
         buf[z] = jnp.concatenate([quads[i].astype(F32) for i in range(4)], axis=0).astype(BF)
-        for n in range(2 - m):
-            ring(m, buf, 0, n).start()
+        for i in range(NP):
+            ring(m, buf, 0, i).start()
         return more
 
     wp_more = begin(0, wpq, wp, wp_y, wp_c)
-    wt_more = begin(1, wtq, wt, wt_y, wt_c)
 
     ri = lax.broadcasted_iota(jnp.int32, (TOK, TOK), 0)
     ci = lax.broadcasted_iota(jnp.int32, (TOK, TOK), 1)
@@ -187,8 +198,10 @@
     same = (clip_r == clip_c) & ((ri % GROUP) == (ci % GROUP))
     mask_ref[...] = jnp.where(same, 1.0, 0.0)
 
+    wt_more = begin(1, wtq, wt, wt_y, wt_c)
     relay(0, wp, 0)
-    ring(1, wt, 0, 1).start()
+    relay(1, wt, 0)
+    relay(0, wp, 1)
 
     def total(buf, n, recv):
         return remote(buf.at[pl.ds(0, n)], buf.at[pl.ds(0, n)], recv, recv, f, s)
@@ -224,20 +237,16 @@
                 remote(att.at[to], attgot.at[s], att_s, att_r, f, to).start()
 
         if i == 1:
-            relay(0, wp, 1)
+            relay(1, wt, 1)
         if i == 3:
-            relay(1, wt, 0, (0,))
+            relay(0, wp, 2)
     attgot[s] = att[s]
 
-    swapped(0, wp, 0)
-    relay(0, wp, 2)
-    relay(1, wt, 0, (1,))
-    swapped(0, wp, 1)
+    for k in range(3):
+        swapped(0, wp, k)
     relay(0, wp, 3)
-    relay(1, wt, 1, (0,))
-    swapped(0, wp, 2)
-    relay(1, wt, 1, (1,))
     swapped(0, wp, 3)
+    relay(1, wt, 2)
 
     total(attgot, NS - 1, att_r).wait_recv()
     rows = jnp.concatenate([attgot[h, :, 0:HD] for h in ORDER], axis=1)
@@ -245,9 +254,10 @@
         for n in range(NC):
             die_arrived(0, wp, k, n).wait_recv()
     projected = jnp.dot(rows, wp[...].reshape(D, D), preferred_element_type=F32)
-    relay(1, wt, 2, (0,))
     hidden = lat_ref[...].astype(F32) + gate_ref[...] * (projected + bias_ref[...])
     hidden_ref[...] = hidden
+    keep = pltpu.make_async_copy(hidden_ref, hidden_out, local.at[6])
+    keep.start()
     mean = jnp.mean(hidden, axis=1, keepdims=True)
     centred = hidden - mean
     variance = jnp.mean(centred * centred, axis=1, keepdims=True)
@@ -264,7 +274,6 @@
     lax.fori_loop(1, NF, send_tok, 0)
     tokgot[f] = toks[group]
 
-    relay(1, wt, 2, (1,))
     swapped(1, wt, 0)
     swapped(1, wt, 1)
     relay(1, wt, 3)
@@ -275,7 +284,7 @@
     for k in range(4):
         for n in range(NC):
             die_arrived(1, wt, k, n).wait_recv()
-    packed = jnp.dot(tokens, wt[...].reshape(D, WT), preferred_element_type=F32).astype(BF)
+    packed = jnp.dot(tokens, wt[...].reshape(D, WIDE), preferred_element_type=F32).astype(BF)
     allowed = mask_ref[...] > 0.5
     parts = []
     for h in range(HEADS // 2):
@@ -304,9 +313,9 @@
         copy.wait_send()
     for m, buf in ((0, wp), (1, wt)):
         for k in range(4):
+            for i in range(NP):
+                ring(m, buf, k, i).wait_send()
             for n in range(NC):
-                if n < 2:
-                    ring(m, buf, k, n).wait_send()
                 die(m, buf, k, n).wait_send()
             swap(m, buf, k, 1).wait_send()
     total(pack, NS - 1, qkv_s).wait_send()
@@ -320,42 +329,56 @@
     for g in range(0, 16, 2):
         pair = [jnp.concatenate([retgot[i].astype(F32), retgot[16 + i].astype(F32)], axis=1) for i in (g, g + 1)]
         out_ref[pl.ds(g * GROUP, 2 * GROUP), :] = jnp.concatenate(pair, axis=0)
+    last = pltpu.make_async_copy(out_ref, temporal_out, local.at[7])
+    last.start()
+    keep.wait()
+    last.wait()
 
 
 def shards(q, k, v, lat, wp, bias, gate, shift, scale, wt, clips):
     flat2 = lambda a: a.reshape(ROWS, D)
     vmem = pl.BlockSpec(memory_space=pltpu.VMEM)
+    hbm = pl.BlockSpec(memory_space=pl.ANY)
     hidden, temporal = pl.pallas_call(
         kernel,
         out_shape=(
             jax.ShapeDtypeStruct((ROWS, D), F32),
             jax.ShapeDtypeStruct((ROWS, D), F32),
         ),
-        in_specs=[pl.BlockSpec(memory_space=pltpu.SMEM)] + [vmem] * 10,
-        out_specs=(vmem, vmem),
+        in_specs=[pl.BlockSpec(memory_space=pltpu.SMEM)] + [hbm] * 6 + [vmem] * 4,
+        out_specs=(hbm, hbm),
         scratch_shapes=[
+            pltpu.VMEM((ROWS, D), BF),
+            pltpu.VMEM((ROWS, D), BF),
+            pltpu.VMEM((ROWS, D), BF),
+            pltpu.VMEM((ROWS, D), BF),
+            pltpu.VMEM((SHARD, D), BF),
+            pltpu.VMEM((SHARD, 3 * D), BF),
+            pltpu.VMEM((ROWS, D), F32),
+            pltpu.VMEM((ROWS, D), F32),
+            pltpu.SemaphoreType.DMA((8,)),
             pltpu.VMEM((NS, ROWS, 256), BF),
             pltpu.VMEM((NS, ROWS, 256), BF),
             pltpu.VMEM((NS, ROWS, 128), BF),
             pltpu.VMEM((NS, ROWS, 128), BF),
             pltpu.VMEM((4, SHARD, D), BF),
-            pltpu.VMEM((4, SHARD, WT), BF),
+            pltpu.VMEM((4, SHARD, WIDE), BF),
             pltpu.VMEM((NZ, QUAD, D), BF),
-            pltpu.VMEM((NZ, QUAD, WT), BF),
+            pltpu.VMEM((NZ, QUAD, WIDE), BF),
             pltpu.VMEM((ROWS // GROUP, GROUP, D), BF),
             pltpu.VMEM((NF, GROUP, D), BF),
             pltpu.VMEM((NF, GROUP, HALF), BF),
             pltpu.VMEM((NF, GROUP, HALF), BF),
             pltpu.VMEM((ROWS, D), F32),
             pltpu.VMEM((TOK, TOK), F32),
-            pltpu.VMEM((SHARD, WT), BF),
+            pltpu.VMEM((SHARD, WIDE), BF),
         ]
         + [pltpu.SemaphoreType.DMA] * 8
         + [
             pltpu.SemaphoreType.DMA((6,)),
             pltpu.SemaphoreType.DMA((6,)),
-            pltpu.SemaphoreType.DMA((8 * NC,)),
-            pltpu.SemaphoreType.DMA((8 * NC,)),
+            pltpu.SemaphoreType.DMA((8 * NP,)),
+            pltpu.SemaphoreType.DMA((8 * NP,)),
             pltpu.SemaphoreType.DMA((8 * NC,)),
             pltpu.SemaphoreType.DMA((8 * NC,)),
             pltpu.SemaphoreType.DMA((8,)),

time: 81.1 us -> 75.5 us (0.931)
  Pallas kernels: 77.8 us -> 72.2 us
    pallas_call x1, Pallas kernels: 77.8 us -> 72.2 us  [shards(): pl.pallas_call(kernel, out_shape=(jax.ShapeDtypeStruct((ROWS, D), F32), j...]
where the time goes in v4:
time: 75.5 us; the launch traced here: 75.3 us
  Pallas kernels  72.2 us (96%)
  local copies, waits for them, and re-layouts  2.46 us (3%)
    pallas_call x1, Pallas kernels, shards(): pl.pallas_call(kernel, out_shape=(jax.ShapeDtypeStruct((ROWS, D), F32), j...  72.2 us
    unnamed x4, local copies, waits for them, and re-layouts  2.46 us

profile of v4, /device:TPU:1, one launch (start us, length us, event | category | flops | bytes accessed | tf_op | source)
XLA Modules:
  0.0 75.3 jit_solution(6855296848378470473)
XLA Ops:
  0.6 72.2 %stdit.1 = (f32[64,1152]{1,0:T(8,128)}, f32[64,1152]{1,0:T(8,128)}) custom-call(s32[16]{0:T(128)} %clip_ref.1, bf16[64,1152]{1,0:T(8,128)(2,1)} %bitcast.8, bf16[64,1152]{1,0:T(8,128)(2,1)} %bitcast.9, bf16[64,1152]{1,0:T(8,128)(2,1)} %bitcast.10, bf16[64,1152]{1,0:T(8,128)(2,1)} %bitcast.11, bf16[36,1152]{1,0:T(8,128)(2,1)} %wp_in.1, ...), custom_call_target="tpu_custom_call" | custom-call | tf_op jit(solution)/shard_map/stdit/pallas_call | solution.py:342
  72.8 0.0 copy-start
  72.8 1.7 %copy.15 = f32[1,64,1152]{2,1,0:T(8,128)} copy(f32[1,64,1152]{2,1,0:T(8,128)} %bitcast.7) | data formatting | bytes 589824
  74.6 0.0 copy-done
  74.6 0.7 copy.16
Async XLA Ops:
  72.8 1.8 %copy-start = (f32[64,1152]{1,0:T(8,128)S(1)}, f32[64,1152]{1,0:T(8,128)}, u32[]{:S(2)}) copy-start(f32[64,1152]{1,0:T(8,128)} %get-tuple-element.5) | copy-start | bytes 884740

commit v5 on v4

--- a/solution.py
+++ b/solution.py
@@ -242,11 +242,12 @@
             relay(0, wp, 2)
     attgot[s] = att[s]
 
-    for k in range(3):
-        swapped(0, wp, k)
+    swapped(0, wp, 0)
+    swapped(0, wp, 1)
     relay(0, wp, 3)
+    relay(1, wt, 2)
+    swapped(0, wp, 2)
     swapped(0, wp, 3)
-    relay(1, wt, 2)
 
     total(attgot, NS - 1, att_r).wait_recv()
     rows = jnp.concatenate([attgot[h, :, 0:HD] for h in ORDER], axis=1)
@@ -254,6 +255,7 @@
         for n in range(NC):
             die_arrived(0, wp, k, n).wait_recv()
     projected = jnp.dot(rows, wp[...].reshape(D, D), preferred_element_type=F32)
+    relay(1, wt, 3)
     hidden = lat_ref[...].astype(F32) + gate_ref[...] * (projected + bias_ref[...])
     hidden_ref[...] = hidden
     keep = pltpu.make_async_copy(hidden_ref, hidden_out, local.at[6])
@@ -276,7 +278,6 @@
 
     swapped(1, wt, 0)
     swapped(1, wt, 1)
-    relay(1, wt, 3)
     swapped(1, wt, 2)
     swapped(1, wt, 3)
     total(tokgot, NF - 1, tok_r).wait_recv()

time: 75.5 us -> 72.5 us (0.960)
  Pallas kernels: 72.2 us -> 69.2 us
    pallas_call x1, Pallas kernels: 72.2 us -> 69.2 us  [shards(): pl.pallas_call(kernel, out_shape=(jax.ShapeDtypeStruct((ROWS, D), F32), j...]
where the time goes in v5:
time: 72.5 us; the launch traced here: 72.3 us
  Pallas kernels  69.2 us (95%)
  local copies, waits for them, and re-layouts  2.46 us (3%)
    pallas_call x1, Pallas kernels, shards(): pl.pallas_call(kernel, out_shape=(jax.ShapeDtypeStruct((ROWS, D), F32), j...  69.2 us
    unnamed x4, local copies, waits for them, and re-layouts  2.46 us

profile of v5, /device:TPU:1, one launch (start us, length us, event | category | flops | bytes accessed | tf_op | source)
XLA Modules:
  0.0 72.3 jit_solution(13252400021023940483)
XLA Ops:
  0.6 69.2 %stdit.1 = (f32[64,1152]{1,0:T(8,128)}, f32[64,1152]{1,0:T(8,128)}) custom-call(s32[16]{0:T(128)} %clip_ref.1, bf16[64,1152]{1,0:T(8,128)(2,1)} %bitcast.8, bf16[64,1152]{1,0:T(8,128)(2,1)} %bitcast.9, bf16[64,1152]{1,0:T(8,128)(2,1)} %bitcast.10, bf16[64,1152]{1,0:T(8,128)(2,1)} %bitcast.11, bf16[36,1152]{1,0:T(8,128)(2,1)} %wp_in.1, ...), custom_call_target="tpu_custom_call" | custom-call | tf_op jit(solution)/shard_map/stdit/pallas_call | solution.py:343
  69.9 0.0 copy-start
  69.9 1.7 %copy.15 = f32[1,64,1152]{2,1,0:T(8,128)} copy(f32[1,64,1152]{2,1,0:T(8,128)} %bitcast.7) | data formatting | bytes 589824
  71.6 0.0 copy-done
  71.6 0.7 copy.16
Async XLA Ops:
  69.9 1.8 %copy-start = (f32[64,1152]{1,0:T(8,128)S(1)}, f32[64,1152]{1,0:T(8,128)}, u32[]{:S(2)}) copy-start(f32[64,1152]{1,0:T(8,128)} %get-tuple-element.5) | copy-start | bytes 884740

commit v6 on v5

--- a/solution.py
+++ b/solution.py
@@ -286,28 +286,34 @@
         for n in range(NC):
             die_arrived(1, wt, k, n).wait_recv()
     packed = jnp.dot(tokens, wt[...].reshape(D, WIDE), preferred_element_type=F32).astype(BF)
-    allowed = mask_ref[...] > 0.5
-    parts = []
-    for h in range(HEADS // 2):
-        qh = packed[:, h * HD : (h + 1) * HD]
-        kh = packed[:, HALF + h * HD : HALF + (h + 1) * HD]
-        vh = packed[:, 2 * HALF + h * HD : 2 * HALF + (h + 1) * HD]
-        scores = lax.dot_general(qh, kh, (((1,), (1,)), ((), ())), preferred_element_type=F32)
-        scores = jnp.where(allowed, scores * (1.0 / math.sqrt(HD)), NEG)
-        top = jnp.max(scores, axis=1, keepdims=True)
-        probs = jnp.exp(scores - top)
-        whole = jnp.sum(probs, axis=1, keepdims=True)
-        parts.append(jnp.dot(probs.astype(BF), vh, preferred_element_type=F32) / whole)
-    mixed = jnp.concatenate(parts, axis=1)
-    for i in range(NF):
-        rets[i] = mixed[i * GROUP : (i + 1) * GROUP].astype(BF)
-
-    def send_ret(i, _):
-        to = (f + i) % NF
-        remote(rets.at[to], retgot.at[f], ret_s, ret_r, to, s).start()
-        return 0
-
-    lax.fori_loop(1, NF, send_ret, 0)
+    allow = mask_ref[...]
+    for half in range(2):
+        rows_of = slice(half * TOK // 2, (half + 1) * TOK // 2)
+        parts = []
+        for h in range(HEADS // 2):
+            qh = packed[rows_of, h * HD : (h + 1) * HD]
+            kh = packed[:, HALF + h * HD : HALF + (h + 1) * HD]
+            vh = packed[:, 2 * HALF + h * HD : 2 * HALF + (h + 1) * HD]
+            scores = lax.dot_general(qh, kh, (((1,), (1,)), ((), ())), preferred_element_type=F32)
+            scores = jnp.where(allow[rows_of] > 0.5, scores * (1.0 / math.sqrt(HD)), NEG)
+            top = jnp.max(scores, axis=1, keepdims=True)
+            probs = jnp.exp(scores - top)
+            whole = jnp.sum(probs, axis=1, keepdims=True)
+            parts.append(jnp.dot(probs.astype(BF), vh, preferred_element_type=F32) / whole)
+        mixed = jnp.concatenate(parts, axis=1)
+        for i in range(NF // 2):
+            rets[half * NF // 2 + i] = mixed[i * GROUP : (i + 1) * GROUP].astype(BF)
+
+        def send_ret(i, _):
+            to = half * (NF // 2) + (f + i) % (NF // 2)
+
+            @pl.when(to != f)
+            def _():
+                remote(rets.at[to], retgot.at[f], ret_s, ret_r, to, s).start()
+
+            return 0
+
+        lax.fori_loop(0, NF // 2, send_ret, 0)
     retgot[f] = rets[f]
 
     for copy in (wp_y, wp_c, wt_y, wt_c, wp_more, wt_more):

time: 72.5 us -> 73.6 us (1.015); the launches traced: 72.3 us -> 72.7 us
  no operation moved by 1% of the time
where the time goes in v6:
time: 73.6 us; the launch traced here: 72.7 us
  Pallas kernels  69.6 us (95%)
  local copies, waits for them, and re-layouts  2.46 us (3%)
    pallas_call x1, Pallas kernels, shards(): pl.pallas_call(kernel, out_shape=(jax.ShapeDtypeStruct((ROWS, D), F32), j...  69.6 us
    unnamed x4, local copies, waits for them, and re-layouts  2.46 us

profile of v6, /device:TPU:1, one launch (start us, length us, event | category | flops | bytes accessed | tf_op | source)
XLA Modules:
  0.0 72.7 jit_solution(7679499472585305333)
XLA Ops:
  0.6 69.6 %stdit.1 = (f32[64,1152]{1,0:T(8,128)}, f32[64,1152]{1,0:T(8,128)}) custom-call(s32[16]{0:T(128)} %clip_ref.1, bf16[64,1152]{1,0:T(8,128)(2,1)} %bitcast.8, bf16[64,1152]{1,0:T(8,128)(2,1)} %bitcast.9, bf16[64,1152]{1,0:T(8,128)(2,1)} %bitcast.10, bf16[64,1152]{1,0:T(8,128)(2,1)} %bitcast.11, bf16[36,1152]{1,0:T(8,128)(2,1)} %wp_in.1, ...), custom_call_target="tpu_custom_call" | custom-call | tf_op jit(solution)/shard_map/stdit/pallas_call | solution.py:349
  70.2 0.0 copy-start
  70.2 1.7 %copy.15 = f32[1,64,1152]{2,1,0:T(8,128)} copy(f32[1,64,1152]{2,1,0:T(8,128)} %bitcast.7) | data formatting | bytes 589824
  72.0 0.0 copy-done
  72.0 0.7 copy.16
Async XLA Ops:
  70.2 1.8 %copy-start = (f32[64,1152]{1,0:T(8,128)S(1)}, f32[64,1152]{1,0:T(8,128)}, u32[]{:S(2)}) copy-start(f32[64,1152]{1,0:T(8,128)} %get-tuple-element.5) | copy-start | bytes 884740
